TPU v7x, 32 devices: a whole 2x2x4 slice. The times are simulated.
32 devices in a mesh: wide: 8 (over y, x, core), narrow: 4 (over z).
Axes of the slice: x: 2, y: 2, z: 4, core: 2. Of those that a mesh axis runs over, the one named last changes fastest.
Arguments:
- image: bfloat16 [2, 256, 256, 256], P(None, 'wide', 'narrow'), may hold values from -6 to 6
- deapodization: float32 [3, 256], replicated, may hold values from 0.5 to 2
- offsets: int32 [32, 8], P(('wide', 'narrow')), may hold values from 0 to 256
- cross_weight: bfloat16 [32, 8, 1536, 1024], P(('wide', 'narrow')), may hold values from -0.1875 to 0.1875
- x_weight: bfloat16 [32, 8, 1536, 256], P(('wide', 'narrow')), may hold values from -0.375 to 0.375
Outputs:
- samples: float32 [32, 8, 2, 1536], P(('wide', 'narrow'))
Inputs may be any that keep to these rules, and one draw needn't show every extreme that they name: `offsets`: each entry is the first row, along the first frequency dimension, of a group's window of 256 rows in one slab.
All inputs are finite; a program needn't handle non-finite values.
Results may differ from a plain program's by a relative error of at most 0.007.
Values may be sent and summed in bfloat16 or wider, within the bound.
A program may use at most 128 MiB of HBM per device.

v0:
```python
import functools
import math

import jax
import jax.numpy as jnp
import numpy as np
from jax import lax
from jax.experimental import pallas as pl
from jax.experimental.pallas import tpu as pltpu
from jax.sharding import PartitionSpec as P

G = 512
KZ = 64
BX = 256


def base_tables(out_rows, inputs, grid_size, lowest):
    frequency = np.arange(out_rows, dtype=np.int64) + lowest
    position = np.arange(inputs, dtype=np.int64) - inputs // 2
    phases = np.mod(frequency[:, None] * position[None, :], grid_size)
    angles = phases.astype(np.float64) * (2.0 * math.pi / grid_size)
    factor = 1.0 / math.sqrt(inputs)
    cosine = (np.cos(angles) * factor).astype(np.float32).astype(jnp.bfloat16)
    sine = (np.sin(angles) * factor).astype(np.float32).astype(jnp.bfloat16)
    return cosine, sine


def complex_table(cosine, sine):
    real_rows = np.stack([cosine, sine], axis=1)
    imag_rows = np.stack([-sine, cosine], axis=1)
    return np.stack([real_rows, imag_rows], axis=0)


def sample_kernel(
    sizes, offsets_ref, band_ref, line_ref, row_ref, x_ref, cross_ref, out_ref, wide_ref, slab_ref, window_ref
):
    depth, grid_rows, width, tile = sizes
    step = pl.program_id(0)
    cells = slab_ref.shape[0]

    @pl.when(step == 0)
    def _():
        def one_plane(k, carry):
            parts = [
                band_ref[:, piece, k].reshape(width, band_ref.shape[-1])
                for piece in range(band_ref.shape[1])
            ]
            plane = jnp.concatenate(parts, axis=-1) if len(parts) > 1 else parts[0]
            lines = lax.dot_general(
                line_ref[...], plane, (((1,), (1,)), ((), ())), preferred_element_type=jnp.float32
            )
            for part in range(2):
                for lane in range(0, width, 128):
                    wide_ref[(part * width + lane) // 128, pl.ds(k, grid_rows, stride=depth), :] = lines[
                        part * grid_rows : (part + 1) * grid_rows, lane : lane + 128
                    ]
            return carry

        for k in range(depth):
            one_plane(k, 0)

    here = pl.ds(pl.multiple_of(step * cells, cells), cells)
    start = offsets_ref[0, step]
    for block in range(2 * width // 128):
        lanes = slice(block * 128, (block + 1) * 128)
        slab_ref[:, lanes] = wide_ref[block, here, :].astype(jnp.bfloat16)
        window_ref[:, lanes] = row_ref[block, pl.ds(start, BX), :].astype(jnp.bfloat16)
    for first in range(0, cross_ref.shape[1], tile):
        rows = slice(first, first + tile)
        partial = jnp.dot(cross_ref[0, rows], slab_ref[...], preferred_element_type=jnp.float32)
        gain = jnp.dot(x_ref[0, rows], window_ref[...], preferred_element_type=jnp.float32)
        part_re, part_im = partial[:, :width], partial[:, width:]
        gain_cos, gain_sin = gain[:, :width], gain[:, width:]
        for part, value in enumerate(
            (gain_cos * part_re + gain_sin * part_im, gain_cos * part_im - gain_sin * part_re)
        ):
            folded = value[:, :128]
            for lane in range(128, width, 128):
                folded = folded + value[:, lane : lane + 128]
            out_ref[0, part : part + 1, rows] = jnp.sum(folded.T, axis=0, keepdims=True)


def gather_kernel(
    wide, narrow, band_ref, out_ref, own_sem, swap_send, swap_recv, chip_send, chip_recv, core_send, core_recv
):
    w = lax.axis_index("wide")
    n = lax.axis_index("narrow")
    sibling = w + 1 - 2 * lax.rem(w, 2)
    chips = wide // 2
    barrier = pltpu.get_barrier_semaphore()
    targets = [(w, lax.rem(n + j, narrow)) for j in range(1, narrow)]
    targets += [(lax.rem(w + 2 * j, wide), n) for j in range(1, chips)] + [(sibling, n)]
    for target in targets:
        pl.semaphore_signal(
            barrier, inc=1, device_id=target, device_id_type=pl.DeviceIdType.MESH
        )
    pl.semaphore_wait(barrier, len(targets))

    def remote(source, place, send, receive, target):
        return pltpu.make_async_remote_copy(
            src_ref=source,
            dst_ref=place,
            send_sem=send,
            recv_sem=receive,
            device_id=target,
            device_id_type=pl.DeviceIdType.MESH,
        )

    swaps = []
    for j in range(1, narrow):
        peer = lax.rem(n + j, narrow)
        swap = remote(
            band_ref.at[peer], out_ref.at[w, n], swap_send.at[j - 1], swap_recv.at[j - 1], (w, peer)
        )
        swap.start()
        swaps.append(swap)
    own = pltpu.make_async_copy(band_ref.at[n], out_ref.at[w, n], own_sem)
    own.start()
    own.wait()
    for swap in swaps:
        swap.wait()
    mine = out_ref.at[w]
    hops = []
    for j in range(1, chips):
        peer = lax.rem(w + 2 * j, wide)
        hop = remote(mine, mine, chip_send.at[j - 1], chip_recv.at[j - 1], (peer, n))
        hop.start()
        hops.append(hop)
    passes = [remote(mine, mine, core_send.at[0], core_recv.at[0], (sibling, n))]
    passes[0].start()
    for j in range(1, chips):
        hops[j - 1].wait_recv()
        block = out_ref.at[lax.rem(w + wide - 2 * j, wide)]
        forward = remote(block, block, core_send.at[j], core_recv.at[j], (sibling, n))
        forward.start()
        passes.append(forward)
    for hop in hops:
        hop.wait_send()
    for forward in passes:
        forward.wait()


def per_device(image, deapodization, offsets, cross_weight, x_weight):
    wide_count = lax.axis_size("wide")
    narrow_count = lax.axis_size("narrow")
    wide_index = lax.axis_index("wide")
    narrow_index = lax.axis_index("narrow")
    block_x = image.shape[1]
    block_y = image.shape[2]
    width = image.shape[3]
    depth = KZ // narrow_count
    samples, cells = cross_weight.shape[2], cross_weight.shape[3]
    scale_x = lax.dynamic_slice_in_dim(deapodization[0], wide_index * block_x, block_x)
    scale_y = lax.dynamic_slice_in_dim(deapodization[1], narrow_index * block_y, block_y)
    weighted = (
        image.astype(jnp.float32)
        * scale_x[None, :, None, None]
        * scale_y[None, None, :, None]
        * deapodization[2][None, None, None, :]
    ).astype(jnp.bfloat16)
    z_table = complex_table(*base_tables(KZ, width, G, -(KZ // 2)))
    band = jnp.einsum(
        "okcz,cxyz->kxoy", jnp.asarray(z_table), weighted, preferred_element_type=jnp.float32
    ).astype(jnp.bfloat16)
    band = band.reshape(KZ, block_x, 2 * block_y)
    band = band.reshape(narrow_count, depth, block_x, 2 * block_y)
    chips = wide_count // 2
    band = pl.pallas_call(
        functools.partial(gather_kernel, wide_count, narrow_count),
        out_shape=jax.ShapeDtypeStruct((wide_count,) + band.shape, band.dtype),
        in_specs=[pl.BlockSpec(memory_space=pltpu.VMEM)],
        out_specs=pl.BlockSpec(memory_space=pltpu.VMEM),
        scratch_shapes=[
            pltpu.SemaphoreType.DMA,
            pltpu.SemaphoreType.DMA((narrow_count - 1,)),
            pltpu.SemaphoreType.DMA((narrow_count - 1,)),
            pltpu.SemaphoreType.DMA((chips - 1,)),
            pltpu.SemaphoreType.DMA((chips - 1,)),
            pltpu.SemaphoreType.DMA((chips,)),
            pltpu.SemaphoreType.DMA((chips,)),
        ],
        compiler_params=pltpu.CompilerParams(collective_id=0, has_side_effects=True),
    )(band)
    if (2 * block_y) % 128:
        band = band.transpose(0, 2, 3, 1, 4).reshape(wide_count, 1, depth, block_x, 2 * width)

    cosine, sine = base_tables(G, width, G, -(G // 2))
    line_table = complex_table(cosine, sine).reshape(2 * G, 2, narrow_count, block_y)
    line_table = line_table.transpose(0, 2, 1, 3).reshape(2 * G, 2 * width)
    row_table = np.concatenate([cosine, sine], axis=1).astype(np.float32)
    row_table = row_table.reshape(G, 2 * width // 128, 128).transpose(1, 0, 2)

    tile = 512 if samples % 512 == 0 else samples
    kernel = functools.partial(sample_kernel, (depth, G, width, tile))
    out = pl.pallas_call(
        kernel,
        grid=(wide_count,),
        out_shape=jax.ShapeDtypeStruct((wide_count, 2, samples), jnp.float32),
        in_specs=[
            pl.BlockSpec(memory_space=pltpu.SMEM),
            pl.BlockSpec(band.shape, lambda s: (0, 0, 0, 0, 0)),
            pl.BlockSpec(line_table.shape, lambda s: (0, 0)),
            pl.BlockSpec(row_table.shape, lambda s: (0, 0, 0)),
            pl.BlockSpec((1, samples, BX), lambda s: (s, 0, 0)),
            pl.BlockSpec((1, samples, cells), lambda s: (s, 0, 0)),
        ],
        out_specs=pl.BlockSpec((1, 2, samples), lambda s: (s, 0, 0)),
        scratch_shapes=[
            pltpu.VMEM((2 * width // 128, G * depth, 128), jnp.float32),
            pltpu.VMEM((cells, 2 * width), jnp.bfloat16),
            pltpu.VMEM((BX, 2 * width), jnp.bfloat16),
        ],
        compiler_params=pltpu.CompilerParams(vmem_limit_bytes=60 * 1024 * 1024),
        cost_estimate=pl.CostEstimate(
            flops=2 * wide_count * samples * 2 * width * (cells + BX) + 8 * G * width * width * depth,
            bytes_accessed=2 * wide_count * samples * (cells + BX),
            transcendentals=0,
        ),
    )(offsets, band, jnp.asarray(line_table), jnp.asarray(row_table), x_weight[0], cross_weight[0])
    return out[None]


def solution(mesh):
    return jax.shard_map(
        per_device,
        mesh=mesh,
        in_specs=(
            P(None, "wide", "narrow", None),
            P(),
            P(("wide", "narrow"), None),
            P(("wide", "narrow"), None, None, None),
            P(("wide", "narrow"), None, None, None),
        ),
        out_specs=P(("wide", "narrow"), None, None, None),
        check_vma=False,
    )
```

profile of v0, /device:TPU:11, one launch (start us, length us, event | category | flops | bytes accessed | tf_op | source)
XLA Modules:
  0.0 83.8 jit_solution(10297580652680264839)
XLA Ops:
  0.0 0.8 fusion.8
  0.8 0.1 dynamic-slice_bitcast_fusion
  0.9 0.1 dynamic-slice_bitcast_fusion.1
  0.9 2.5 %fusion.5 = bf16[64,32,2,64]{0,3,2,1:T(8,128)(2,1)S(1)} fusion(bf16[2,64,2,256,1]{3,1,2,0,4:T(8,128)(2,1)} %constant.31, bf16[2,32,64,256]{3,2,1,0:T(8,128)(2,1)} %param.8, f32[256]{0:T(256)S(1)} %bitcast.21, f32[64]{0:T(128)S(1)} %dynamic-slice_bitcast_fusion, f32[32]{0:T(128)S(1)} %dynamic-slice_bitcast_fusion.1), kind=kOutput, calls=%fused_computation.5 | convolution fusion | flops 273940480 | bytes 2753920 | tf_op jit(solution)/shard_map/okcz,cxyz->kxoy/dot_general | solution.py:162
  3.5 1.1 %copy.10 = bf16[64,32,2,64]{3,2,1,0:T(2,128)(2,1)S(1)} copy(bf16[64,32,2,64]{0,3,2,1:T(8,128)(2,1)S(1)} %fusion.5) | data formatting | bytes 1048576 | tf_op jit(solution)/shard_map/convert_element_type | solution.py:164
  4.6 1.3 %reshape_reshape.3.band_ref = bf16[4,16,32,128]{3,2,1,0:T(8,128)(2,1)} reshape(bf16[64,32,2,64]{3,2,1,0:T(2,128)(2,1)S(1)} %copy.10) | data formatting | bytes 1048576 | tf_op jit(solution)/shard_map/reshape;reshape | solution.py:166
  5.8 45.3 %shard_map.82.band_ref = bf16[8,4,16,32,128]{4,3,2,1,0:T(8,128)(2,1)} custom-call(bf16[4,16,32,128]{3,2,1,0:T(8,128)(2,1)} %reshape_reshape.3.band_ref), custom_call_target="tpu_custom_call" | custom-call | tf_op jit(solution)/shard_map/pallas_call | solution.py:168
  51.1 32.7 %shard_map.83 = f32[8,2,1536]{2,1,0:T(2,128)} custom-call(s32[1,8]{1,0:T(1,128)} %offsets_ref.1, bf16[8,4,16,32,128]{4,3,2,1,0:T(8,128)(2,1)} %shard_map.82.band_ref, bf16[1024,512]{1,0:T(8,128)(2,1)} %constant.26.clone.line_ref, f32[4,512,128]{2,1,0:T(8,128)} %constant.27.clone.row_ref, bf16[8,1536,256]{2,1,0:T(8,128)(2,1)} %bitcast.23, ...), custom_call_target="tpu_custom_call" | custom-call | flops 20401094656 | bytes 31457280 | tf_op jit(solution)/shard_map/pallas_call | solution.py:195
where the time goes:
time: 84.1 us; the launch traced here: 83.8 us
  Pallas kernels  78 us (93%)
  local copies, waits for them, and re-layouts  3.3 us (4%)
  matrix products  2.53 us (3%)
    pallas_call x1, Pallas kernels, per_device(): pl.pallas_call(functools.partial(gather_kernel, wide_count, narrow_count)...  45.3 us
    pallas_call x1, Pallas kernels, per_device(): pl.pallas_call(kernel, grid=(wide_count,), out_shape=jax.ShapeDtypeStruct...  32.7 us
    dot_general x1, matrix products, per_device(): jnp.einsum('okcz,cxyz->kxoy', jnp.asarray(z_table), weighted, preferred_e...  2.53 us

commit v1 on v0

--- a/solution.py
+++ b/solution.py
@@ -220,9 +220,377 @@
     return out[None]
 
 
+def flip(index, bits):
+    low = lax.rem(index + bits, 2)
+    high = lax.rem(lax.div(index, 2) + lax.div(bits, 2), 2)
+    return low + 2 * high
+
+
+def fused_kernel(
+    sizes, image_hbm, deap_smem, deap_ref, offsets_ref, z_hbm, line_hbm, row_hbm, x_hbm, cross_hbm, out_ref,
+    image_ref, scale_ref, spread_ref, send_ref, grid_ref, z_ref, line_ref, row_ref, x_ref, window_ref, gain_ref,
+    cross_ref, wide_ref, slab_a, slab_b,
+    image_sem, table_sem, x_sem, cross_sem,
+    swap_send, swap_recv, own_send, near_recv, relay_send, relay_recv, pass_send, pass_recv,
+):
+    depth, grid_rows, tile = sizes
+    w = lax.axis_index("wide")
+    n = lax.axis_index("narrow")
+    rounds, narrow, wide, _, strip, lanes = grid_ref.shape
+    slots = x_ref.shape[0]
+    block_y, width = scale_ref.shape
+    slabs, samples, cells = cross_ref.shape
+    pitch = depth + 1
+    half = wide * strip
+    span = cells // depth
+
+    core = lax.rem(w, 2)
+    across = w + 2 - 4 * lax.rem(lax.div(w, 2), 2)
+    along = w + 4 - 8 * lax.rem(lax.div(w, 4), 2)
+    first = across + core * (along - across)
+    second = along + core * (across - along)
+    corner = across + along - w
+    sibling = w + 1 - 2 * core
+    held = (w, first, second, corner)
+    sib_across = across + 1 - 2 * core
+    sib_along = along + 1 - 2 * core
+    sib_first = sib_along + core * (sib_across - sib_along)
+    sib_second = sib_across + core * (sib_along - sib_across)
+    theirs = (sibling, sib_first, sib_second, corner + 1 - 2 * core)
+
+    def remote(source, place, send, receive, target):
+        return pltpu.make_async_remote_copy(
+            src_ref=source, dst_ref=place, send_sem=send, recv_sem=receive,
+            device_id=target, device_id_type=pl.DeviceIdType.MESH,
+        )
+
+    image_loads = [
+        pltpu.make_async_copy(
+            image_hbm.at[:, r * strip : (r + 1) * strip],
+            image_ref.at[:, r * strip : (r + 1) * strip],
+            image_sem.at[r],
+        )
+        for r in range(rounds)
+    ]
+    table_loads = [
+        pltpu.make_async_copy(source, place, table_sem.at[i])
+        for i, (source, place) in enumerate(((z_hbm, z_ref), (row_hbm, row_ref), (line_hbm, line_ref)))
+    ]
+
+    def x_load(s):
+        return pltpu.make_async_copy(x_hbm.at[s], x_ref.at[s % slots], x_sem.at[s % slots])
+
+    def cross_load(s):
+        return pltpu.make_async_copy(cross_hbm.at[s], cross_ref.at[s], cross_sem.at[s])
+
+    image_loads[0].start()
+    table_loads[0].start()
+    image_loads[1].start()
+    barrier = pltpu.get_barrier_semaphore()
+    peers = [(w, flip(n, j)) for j in range(1, narrow)] + [(first, n), (second, n), (sibling, n)]
+    for peer in peers:
+        pl.semaphore_signal(barrier, inc=1, device_id=peer, device_id_type=pl.DeviceIdType.MESH)
+
+    last = deap_ref[2:3, :]
+    for y in range(block_y):
+        scale_ref[y : y + 1, :] = last * deap_smem[1, n * block_y + y]
+
+    def band(r):
+        low = lax.broadcasted_iota(jnp.int32, (narrow * depth, lanes), 1) < block_y
+        group = width // block_y
+        for at in range(0, strip, group):
+            halves = []
+            for c in range(2):
+                pieces = []
+                for x in range(at, at + group):
+                    gain = scale_ref[...] * deap_smem[0, w * rounds * strip + r * strip + x]
+                    pieces.append((image_ref[c, r * strip + x].astype(jnp.float32) * gain).astype(jnp.bfloat16))
+                halves.append(jnp.concatenate(pieces, axis=0))
+            both = jnp.concatenate(halves, axis=1)
+            value = lax.dot_general(z_ref[...], both, (((1,), (1,)), ((), ())), preferred_element_type=jnp.float32)
+            real, imag = value[: narrow * depth], value[narrow * depth :]
+            for pair in range(group // 2):
+                here = slice(pair * lanes, (pair + 1) * lanes)
+                even = jnp.where(low, real[:, here], pltpu.roll(imag[:, here], block_y, 1))
+                odd = jnp.where(low, pltpu.roll(real[:, here], block_y, 1), imag[:, here])
+                spread_ref[pl.ds(at + 2 * pair, narrow * depth, stride=pitch), :] = even
+                spread_ref[pl.ds(at + 2 * pair + 1, narrow * depth, stride=pitch), :] = odd
+        for k in range(narrow * depth):
+            send_ref[r, k // depth, k % depth] = spread_ref[k * pitch : k * pitch + strip, :].astype(jnp.bfloat16)
+        grid_ref[r, n, w] = send_ref[r, n]
+
+    def swap(r, j):
+        peer = flip(n, j)
+        return remote(
+            send_ref.at[r, peer], grid_ref.at[r, n, w], swap_send.at[r, j], swap_recv.at[r, j], (w, peer)
+        )
+
+    def place(r, j, column):
+        return grid_ref.at[r, flip(n, j), column]
+
+    def own_copies(r, j):
+        mine = place(r, j, w)
+        return [
+            remote(mine, mine, own_send.at[r, j, 0], near_recv.at[r, j, 0], (first, n)),
+            remote(mine, mine, own_send.at[r, j, 1], near_recv.at[r, j, 1], (second, n)),
+            pass_copy(r, j, 0),
+        ]
+
+    def relay_copy(r, j):
+        block = place(r, j, first)
+        return remote(block, block, relay_send.at[r, j], relay_recv.at[r, j], (second, n))
+
+    def pass_copy(r, j, kind):
+        block = place(r, j, held[kind])
+        return remote(block, block, pass_send.at[r, j, kind], pass_recv.at[r, j, kind], (sibling, n))
+
+    def arrived(r, j, column, send, receive):
+        block = place(r, j, column)
+        remote(block, block, send, receive, (sibling, n)).wait_recv()
+
+    def own(r, j):
+        if j > 0:
+            block = grid_ref.at[r, flip(n, j), w]
+            remote(block, block, swap_send.at[r, j], swap_recv.at[r, j], (w, flip(n, j))).wait_recv()
+        for copy in own_copies(r, j):
+            copy.start()
+
+    def relay(r, j):
+        arrived(r, j, first, own_send.at[r, j, 0], near_recv.at[r, j, 0])
+        relay_copy(r, j).start()
+        pass_copy(r, j, 1).start()
+
+    def near(r, j):
+        arrived(r, j, second, own_send.at[r, j, 1], near_recv.at[r, j, 1])
+        pass_copy(r, j, 2).start()
+
+    def far(r, j):
+        arrived(r, j, corner, relay_send.at[r, j], relay_recv.at[r, j])
+        pass_copy(r, j, 3).start()
+
+    def settle(r):
+        for j in range(narrow):
+            for kind in range(4):
+                arrived(r, j, theirs[kind], pass_send.at[r, j, kind], pass_recv.at[r, j, kind])
+
+    def gains(s):
+        x_load(s).wait()
+        start = offsets_ref[0, s]
+        for block in range(row_ref.shape[0]):
+            window_ref[:, block * 128 : (block + 1) * 128] = row_ref[block, pl.ds(start, BX), :].astype(jnp.bfloat16)
+        for at in range(0, samples, tile):
+            rows = slice(at, at + tile)
+            gain_ref[s, rows] = jnp.dot(
+                x_ref[s % slots, rows], window_ref[...], preferred_element_type=jnp.float32
+            ).astype(jnp.bfloat16)
+        if s + slots < slabs:
+            x_load(s + slots).start()
+
+    def lines(r, k):
+        planes = [
+            jnp.concatenate([grid_ref[r, source, :, k + i].reshape(half, lanes) for i in range(2)], axis=0)
+            for source in range(narrow)
+        ]
+        plane = jnp.concatenate(planes, axis=1)
+        value = lax.dot_general(
+            line_ref[...], plane, (((1,), (1,)), ((), ())), preferred_element_type=jnp.float32
+        )
+        for part in range(2):
+            for i in range(2):
+                wide_ref[part, pl.ds(k + i, grid_rows, stride=pitch), :] = value[
+                    part * grid_rows : (part + 1) * grid_rows, i * half : (i + 1) * half
+                ]
+
+    def gather(s, slab_ref):
+        base = s * span * pitch
+        for part in range(2):
+            for y in range(span):
+                slab_ref[y * depth : (y + 1) * depth, part * half : (part + 1) * half] = wide_ref[
+                    part, pl.ds(base + y * pitch, depth), :
+                ].astype(jnp.bfloat16)
+
+    def contract(r, s, slab_ref):
+        for at in range(0, samples, tile):
+            rows = slice(at, at + tile)
+            value = jnp.dot(cross_ref[s, rows], slab_ref[...], preferred_element_type=jnp.float32)
+            real, imag = value[:, :half], value[:, half:]
+            gain = gain_ref[s, rows, 2 * r * half : 2 * (r + 1) * half].astype(jnp.float32)
+            cosine, sine = gain[:, :half], gain[:, half:]
+            for part, product in enumerate((cosine * real + sine * imag, cosine * imag - sine * real)):
+                total = jnp.sum(product.T, axis=0, keepdims=True)
+                if r > 0:
+                    total = total + out_ref[s, part : part + 1, rows]
+                out_ref[s, part : part + 1, rows] = total
+
+    for copy in table_loads[1:]:
+        copy.start()
+    for s in range(slots):
+        x_load(s).start()
+    table_loads[0].wait()
+    image_loads[0].wait()
+    band(0)
+    for s in range(slabs):
+        cross_load(s).start()
+    pl.semaphore_wait(barrier, len(peers))
+    for j in range(1, narrow):
+        swap(0, j).start()
+    own(0, 0)
+    image_loads[1].wait()
+    band(1)
+    for j in range(1, narrow):
+        swap(1, j).start()
+    table_loads[1].wait()
+    table_loads[2].wait()
+    for s in range(4):
+        gains(s)
+    relay(0, 0)
+    own(0, 1)
+    for s in range(4, 6):
+        gains(s)
+    near(0, 0)
+    far(0, 0)
+    for s in range(6, slabs):
+        gains(s)
+    relay(0, 1)
+    own(0, 2)
+    near(0, 1)
+    own(0, 3)
+    relay(0, 2)
+    far(0, 1)
+    own(1, 0)
+    near(0, 2)
+    relay(0, 3)
+    far(0, 2)
+    near(0, 3)
+    own(1, 1)
+    far(0, 3)
+    relay(1, 0)
+    settle(0)
+
+    events = {
+        1: [(near, 0), (own, 2)],
+        3: [(far, 0), (relay, 1)],
+        5: [(near, 1), (own, 3)],
+        7: [(far, 1), (relay, 2)],
+    }
+    for pair in range(depth // 2):
+        lines(0, 2 * pair)
+        for event, j in events.get(pair, []):
+            event(1, j)
+    for s in range(slabs):
+        cross_load(s).wait()
+
+    gather(0, slab_a)
+
+    def steps(r, i):
+        gather(2 * i + 1, slab_b)
+        contract(r, 2 * i, slab_a)
+        gather(lax.rem(2 * i + 2, slabs), slab_a)
+        contract(r, 2 * i + 1, slab_b)
+
+    def early(i, carry):
+        steps(0, i)
+        return carry
+
+    def late(i, carry):
+        steps(1, i)
+        return carry
+
+    lax.fori_loop(0, 1, early, 0)
+    near(1, 2)
+    relay(1, 3)
+    lax.fori_loop(1, 2, early, 0)
+    far(1, 2)
+    near(1, 3)
+    lax.fori_loop(2, 3, early, 0)
+    far(1, 3)
+    lax.fori_loop(3, slabs // 2, early, 0)
+    settle(1)
+    for pair in range(depth // 2):
+        lines(1, 2 * pair)
+    gather(0, slab_a)
+    lax.fori_loop(0, slabs // 2, late, 0)
+
+    for r in range(rounds):
+        for j in range(narrow):
+            if j > 0:
+                swap(r, j).wait_send()
+            for copy in own_copies(r, j):
+                copy.wait_send()
+            relay_copy(r, j).wait_send()
+            for kind in range(1, 4):
+                pass_copy(r, j, kind).wait_send()
+
+
+def fused_device(image, deapodization, offsets, cross_weight, x_weight):
+    wide = lax.axis_size("wide")
+    narrow = lax.axis_size("narrow")
+    block_x, block_y, width = image.shape[1:]
+    depth = KZ // narrow
+    slabs, samples, cells = cross_weight.shape[1:]
+    rounds = 2
+    strip = block_x // rounds
+    lanes = 2 * block_y
+    slots = 4
+    z_table = complex_table(*base_tables(KZ, width, G, -(KZ // 2))).reshape(2 * KZ, 2 * width)
+    cosine, sine = base_tables(G, width, G, -(G // 2))
+    line_table = complex_table(cosine, sine).reshape(2 * G, 2, narrow, block_y)
+    line_table = line_table.transpose(0, 2, 1, 3).reshape(2 * G, 2 * width)
+    row_table = np.stack([cosine, sine], axis=0).astype(np.float32).reshape(2, G, wide, rounds, strip)
+    row_table = row_table.transpose(3, 0, 1, 2, 4).reshape(2 * rounds, G, wide * strip)
+    hbm = pl.BlockSpec(memory_space=pl.ANY)
+    vmem = pl.BlockSpec(memory_space=pltpu.VMEM)
+    smem = pl.BlockSpec(memory_space=pltpu.SMEM)
+    dma = pltpu.SemaphoreType.DMA
+    half = wide * strip
+    out = pl.pallas_call(
+        functools.partial(fused_kernel, (depth, G, 512 if samples % 512 == 0 else samples)),
+        out_shape=jax.ShapeDtypeStruct((slabs, 2, samples), jnp.float32),
+        in_specs=[hbm, smem, vmem, smem, hbm, hbm, hbm, hbm, hbm],
+        out_specs=vmem,
+        scratch_shapes=[
+            pltpu.VMEM(image.shape, jnp.bfloat16),
+            pltpu.VMEM((block_y, width), jnp.float32),
+            pltpu.VMEM((KZ * (depth + 1), lanes), jnp.float32),
+            pltpu.VMEM((rounds, narrow, depth, strip, lanes), jnp.bfloat16),
+            pltpu.VMEM((rounds, narrow, wide, depth, strip, lanes), jnp.bfloat16),
+            pltpu.VMEM(z_table.shape, jnp.bfloat16),
+            pltpu.VMEM(line_table.shape, jnp.bfloat16),
+            pltpu.VMEM(row_table.shape, jnp.float32),
+            pltpu.VMEM((slots, samples, BX), jnp.bfloat16),
+            pltpu.VMEM((BX, 2 * width), jnp.bfloat16),
+            pltpu.VMEM((slabs, samples, 2 * width), jnp.bfloat16),
+            pltpu.VMEM((slabs, samples, cells), jnp.bfloat16),
+            pltpu.VMEM((2, G * (depth + 1), half), jnp.float32),
+            pltpu.VMEM((cells, 2 * half), jnp.bfloat16),
+            pltpu.VMEM((cells, 2 * half), jnp.bfloat16),
+            dma((rounds,)),
+            dma((3,)),
+            dma((slots,)),
+            dma((slabs,)),
+            dma((rounds, narrow)),
+            dma((rounds, narrow)),
+            dma((rounds, narrow, 2)),
+            dma((rounds, narrow, 2)),
+            dma((rounds, narrow)),
+            dma((rounds, narrow)),
+            dma((rounds, narrow, 4)),
+            dma((rounds, narrow, 4)),
+        ],
+        compiler_params=pltpu.CompilerParams(
+            vmem_limit_bytes=67043328, collective_id=1, has_side_effects=True
+        ),
+    )(
+        image, deapodization, deapodization, offsets, jnp.asarray(z_table), jnp.asarray(line_table),
+        jnp.asarray(row_table), x_weight[0], cross_weight[0],
+    )
+    return out[None]
+
+
 def solution(mesh):
+    square = mesh.shape["wide"] == 8 and mesh.shape["narrow"] == 4
     return jax.shard_map(
-        per_device,
+        fused_device if square else per_device,
         mesh=mesh,
         in_specs=(
             P(None, "wide", "narrow", None),

time: 84.1 us -> 56.9 us (0.68)
  the two profiles are of different devices: /device:TPU:11 before, /device:TPU:0 now
where the time goes in v1:
time: 56.9 us; the launch traced here: 56.7 us
  Pallas kernels  55.2 us (97%)
  local copies, waits for them, and re-layouts  1.54 us (3%)
    pallas_call x1, Pallas kernels, fused_device(): pl.pallas_call(functools.partial(fused_kernel, (depth, G, 512 if samples...  55.2 us
    unnamed x1, local copies, waits for them, and re-layouts  1.54 us

profile of v1, /device:TPU:0, one launch (start us, length us, event | category | flops | bytes accessed | tf_op | source)
XLA Modules:
  0.0 56.7 jit_solution(17333698871802761310)
XLA Ops:
  0.0 55.2 %shard_map.82 = f32[8,2,1536]{2,1,0:T(2,128)} custom-call(bf16[2,32,64,256]{3,2,1,0:T(8,128)(2,1)} %image_hbm.1, f32[3,256]{1,0:T(4,128)} %deap_ref.1, f32[3,256]{1,0:T(4,128)} %deap_ref.1, s32[1,8]{1,0:T(1,128)} %offsets_ref.1, bf16[128,512]{1,0:T(8,128)(2,1)} %constant.6.clone.z_hbm, bf16[1024,512]{1,0:T(8,128)(2,1)} %constant.7.clone.line_hbm, ...), custom_call_target="tpu_custom_call" | custom-call | tf_op jit(solution)/shard_map/pallas_call | solution.py:546
  55.2 1.5 %copy.10 = f32[1,8,2,1536]{3,2,1,0:T(2,128)} copy(f32[1,8,2,1536]{3,2,1,0:T(2,128)} %bitcast.5) | data formatting | bytes 196608

commit v2 on v1

--- a/solution.py
+++ b/solution.py
@@ -12,6 +12,7 @@
 G = 512
 KZ = 64
 BX = 256
+TILE = 128
 
 
 def base_tables(out_rows, inputs, grid_size, lowest):
@@ -227,16 +228,17 @@
 
 
 def fused_kernel(
-    sizes, image_hbm, deap_smem, deap_ref, offsets_ref, z_hbm, line_hbm, row_hbm, x_hbm, cross_hbm, out_ref,
-    image_ref, scale_ref, spread_ref, send_ref, grid_ref, z_ref, line_ref, row_ref, x_ref, window_ref, gain_ref,
+    sizes, image_hbm, deap_hbm, offsets_hbm, z_hbm, line_hbm, row_hbm, x_hbm, cross_hbm, out_ref,
+    deap_smem, deap_ref, offsets_ref, image_ref, scale_ref, perm_ref, spread_ref, send_ref, grid_ref, z_ref, line_ref, packed_ref, row_ref, x_ref, window_a, window_b, gain_ref,
     cross_ref, wide_ref, slab_a, slab_b,
-    image_sem, table_sem, x_sem, cross_sem,
+    small_sem, image_sem, table_sem, x_sem, cross_sem,
     swap_send, swap_recv, own_send, near_recv, relay_send, relay_recv, pass_send, pass_recv,
 ):
     depth, grid_rows, tile = sizes
     w = lax.axis_index("wide")
     n = lax.axis_index("narrow")
     rounds, narrow, wide, _, strip, lanes = grid_ref.shape
+    windows = (window_a, window_b)
     slots = x_ref.shape[0]
     block_y, width = scale_ref.shape
     slabs, samples, cells = cross_ref.shape
@@ -252,6 +254,7 @@
     corner = across + along - w
     sibling = w + 1 - 2 * core
     held = (w, first, second, corner)
+    straight = ((0, 3),)
     sib_across = across + 1 - 2 * core
     sib_along = along + 1 - 2 * core
     sib_first = sib_along + core * (sib_across - sib_along)
@@ -274,7 +277,7 @@
     ]
     table_loads = [
         pltpu.make_async_copy(source, place, table_sem.at[i])
-        for i, (source, place) in enumerate(((z_hbm, z_ref), (row_hbm, row_ref), (line_hbm, line_ref)))
+        for i, (source, place) in enumerate(((z_hbm, z_ref), (row_hbm, packed_ref), (line_hbm, line_ref)))
     ]
 
     def x_load(s):
@@ -283,36 +286,56 @@
     def cross_load(s):
         return pltpu.make_async_copy(cross_hbm.at[s], cross_ref.at[s], cross_sem.at[s])
 
+    small_loads = [
+        pltpu.make_async_copy(source, place, small_sem.at[i])
+        for i, (source, place) in enumerate(((deap_hbm, deap_smem), (deap_hbm, deap_ref), (offsets_hbm, offsets_ref)))
+    ]
+    for copy in small_loads:
+        copy.start()
     image_loads[0].start()
     table_loads[0].start()
     image_loads[1].start()
     barrier = pltpu.get_barrier_semaphore()
-    peers = [(w, flip(n, j)) for j in range(1, narrow)] + [(first, n), (second, n), (sibling, n)]
+    peers = [(w, flip(n, j)) for j in range(1, narrow)] + [(first, n), (second, n), (corner, n), (sibling, n)]
     for peer in peers:
         pl.semaphore_signal(barrier, inc=1, device_id=peer, device_id_type=pl.DeviceIdType.MESH)
 
+    row_at = lax.broadcasted_iota(jnp.int32, perm_ref.shape, 0)
+    lane_at = lax.broadcasted_iota(jnp.int32, perm_ref.shape, 1)
+    parity_at = lax.rem(lax.div(lax.rem(lane_at, lanes), block_y) + n, 2)
+    line_at = lax.div(lax.rem(lane_at, block_y), block_y // 2)
+    source_at = lax.div(lane_at, lanes) * lanes + line_at * block_y + 2 * lax.rem(lane_at, block_y // 2) + parity_at
+    perm_ref[...] = jnp.where(row_at == source_at, 1.0, 0.0).astype(jnp.bfloat16)
+    for copy in small_loads:
+        copy.wait()
     last = deap_ref[2:3, :]
     for y in range(block_y):
         scale_ref[y : y + 1, :] = last * deap_smem[1, n * block_y + y]
 
     def band(r):
-        low = lax.broadcasted_iota(jnp.int32, (narrow * depth, lanes), 1) < block_y
+        quarter = block_y // 2
+        low = lax.rem(lax.broadcasted_iota(jnp.int32, (narrow * depth, lanes), 1), block_y) < quarter
         group = width // block_y
+        rows = 2 * narrow * depth
+        halves = []
+        for c in range(2):
+            pieces = []
+            for x in range(strip):
+                gain = scale_ref[...] * deap_smem[0, w * rounds * strip + r * strip + x]
+                pieces.append((image_ref[c, r * strip + x].astype(jnp.float32) * gain).astype(jnp.bfloat16))
+            halves.append(jnp.concatenate(pieces, axis=0))
+        both = jnp.concatenate(halves, axis=1)
+        value = lax.dot_general(z_ref[...], both, (((1,), (1,)), ((), ())), preferred_element_type=jnp.float32)
+        value = value.astype(jnp.bfloat16)
+        value = jnp.concatenate([value[:, at : at + width] for at in range(0, strip * block_y, width)], axis=0)
+        value = jnp.dot(value, perm_ref[...], preferred_element_type=jnp.float32)
         for at in range(0, strip, group):
-            halves = []
-            for c in range(2):
-                pieces = []
-                for x in range(at, at + group):
-                    gain = scale_ref[...] * deap_smem[0, w * rounds * strip + r * strip + x]
-                    pieces.append((image_ref[c, r * strip + x].astype(jnp.float32) * gain).astype(jnp.bfloat16))
-                halves.append(jnp.concatenate(pieces, axis=0))
-            both = jnp.concatenate(halves, axis=1)
-            value = lax.dot_general(z_ref[...], both, (((1,), (1,)), ((), ())), preferred_element_type=jnp.float32)
-            real, imag = value[: narrow * depth], value[narrow * depth :]
+            real = value[at // group * rows : at // group * rows + rows // 2]
+            imag = value[at // group * rows + rows // 2 : (at // group + 1) * rows]
             for pair in range(group // 2):
                 here = slice(pair * lanes, (pair + 1) * lanes)
-                even = jnp.where(low, real[:, here], pltpu.roll(imag[:, here], block_y, 1))
-                odd = jnp.where(low, pltpu.roll(real[:, here], block_y, 1), imag[:, here])
+                even = jnp.where(low, real[:, here], pltpu.roll(imag[:, here], quarter, 1))
+                odd = jnp.where(low, pltpu.roll(real[:, here], lanes - quarter, 1), imag[:, here])
                 spread_ref[pl.ds(at + 2 * pair, narrow * depth, stride=pitch), :] = even
                 spread_ref[pl.ds(at + 2 * pair + 1, narrow * depth, stride=pitch), :] = odd
         for k in range(narrow * depth):
@@ -337,8 +360,9 @@
         ]
 
     def relay_copy(r, j):
-        block = place(r, j, first)
-        return remote(block, block, relay_send.at[r, j], relay_recv.at[r, j], (second, n))
+        column, target = (w, corner) if (r, j) in straight else (first, second)
+        block = place(r, j, column)
+        return remote(block, block, relay_send.at[r, j], relay_recv.at[r, j], (target, n))
 
     def pass_copy(r, j, kind):
         block = place(r, j, held[kind])
@@ -354,10 +378,13 @@
             remote(block, block, swap_send.at[r, j], swap_recv.at[r, j], (w, flip(n, j))).wait_recv()
         for copy in own_copies(r, j):
             copy.start()
+        if (r, j) in straight:
+            relay_copy(r, j).start()
 
     def relay(r, j):
         arrived(r, j, first, own_send.at[r, j, 0], near_recv.at[r, j, 0])
-        relay_copy(r, j).start()
+        if (r, j) not in straight:
+            relay_copy(r, j).start()
         pass_copy(r, j, 1).start()
 
     def near(r, j):
@@ -373,33 +400,47 @@
             for kind in range(4):
                 arrived(r, j, theirs[kind], pass_send.at[r, j, kind], pass_recv.at[r, j, kind])
 
-    def gains(s):
-        x_load(s).wait()
-        start = offsets_ref[0, s]
-        for block in range(row_ref.shape[0]):
-            window_ref[:, block * 128 : (block + 1) * 128] = row_ref[block, pl.ds(start, BX), :].astype(jnp.bfloat16)
-        for at in range(0, samples, tile):
-            rows = slice(at, at + tile)
-            gain_ref[s, rows] = jnp.dot(
-                x_ref[s % slots, rows], window_ref[...], preferred_element_type=jnp.float32
-            ).astype(jnp.bfloat16)
-        if s + slots < slabs:
-            x_load(s + slots).start()
+    def gains(*batch):
+        for s in batch:
+            x_load(s).wait()
+        for s, window in zip(batch, windows):
+            start = offsets_ref[0, s]
+            for block in range(row_ref.shape[0]):
+                window[:, block * 128 : (block + 1) * 128] = row_ref[block, pl.ds(start, BX), :].astype(jnp.bfloat16)
+            for at in range(0, samples, 512):
+                rows = slice(at, at + 512)
+                gain_ref[s, rows] = jnp.dot(
+                    x_ref[s % slots, rows], window[...], preferred_element_type=jnp.float32
+                ).astype(jnp.bfloat16)
+        for s in batch:
+            if s + slots < slabs:
+                x_load(s + slots).start()
+        for s in batch:
+            cross_load(s).start()
 
     def lines(r, k):
+        low = lax.broadcasted_iota(jnp.int32, (2 * half, lanes), 1) < block_y
         planes = [
             jnp.concatenate([grid_ref[r, source, :, k + i].reshape(half, lanes) for i in range(2)], axis=0)
             for source in range(narrow)
         ]
-        plane = jnp.concatenate(planes, axis=1)
-        value = lax.dot_general(
-            line_ref[...], plane, (((1,), (1,)), ((), ())), preferred_element_type=jnp.float32
-        )
-        for part in range(2):
-            for i in range(2):
-                wide_ref[part, pl.ds(k + i, grid_rows, stride=pitch), :] = value[
-                    part * grid_rows : (part + 1) * grid_rows, i * half : (i + 1) * half
-                ]
+        evens, odds = [], []
+        for one, two in zip(planes[::2], planes[1::2]):
+            evens.append(jnp.where(low, one, two))
+            odds.append(jnp.where(low, two, one))
+        even, odd = [
+            lax.dot_general(
+                line_ref[parity], jnp.concatenate(pieces, axis=1), (((1,), (1,)), ((), ())),
+                preferred_element_type=jnp.float32,
+            )
+            for parity, pieces in enumerate((evens, odds))
+        ]
+        for sign, value in enumerate((even + odd, even - odd)):
+            for part in range(2):
+                for i in range(2):
+                    wide_ref[part, pl.ds(sign * (grid_rows // 2) * pitch + k + i, grid_rows // 2, stride=pitch), :] = value[
+                        part * grid_rows // 2 : (part + 1) * grid_rows // 2, i * half : (i + 1) * half
+                    ]
 
     def gather(s, slab_ref):
         base = s * span * pitch
@@ -429,58 +470,53 @@
     table_loads[0].wait()
     image_loads[0].wait()
     band(0)
-    for s in range(slabs):
-        cross_load(s).start()
     pl.semaphore_wait(barrier, len(peers))
     for j in range(1, narrow):
         swap(0, j).start()
     own(0, 0)
     image_loads[1].wait()
     band(1)
+    own(1, 0)
+    table_loads[1].wait()
+    row_ref[...] = packed_ref[...].astype(jnp.float32)
+    gains(0, 1)
+    relay(0, 0)
+    own(0, 1)
+    gains(2, 3)
+    near(0, 0)
+    own(0, 2)
+    gains(4, 5)
+    own(0, 3)
     for j in range(1, narrow):
         swap(1, j).start()
-    table_loads[1].wait()
-    table_loads[2].wait()
-    for s in range(4):
-        gains(s)
-    relay(0, 0)
-    own(0, 1)
-    for s in range(4, 6):
-        gains(s)
-    near(0, 0)
+    relay(0, 1)
+    near(0, 1)
     far(0, 0)
-    for s in range(6, slabs):
-        gains(s)
-    relay(0, 1)
-    own(0, 2)
-    near(0, 1)
-    own(0, 3)
+    gains(6, 7)
     relay(0, 2)
-    far(0, 1)
-    own(1, 0)
     near(0, 2)
     relay(0, 3)
+    near(0, 3)
+    far(0, 1)
+    relay(1, 0)
+    near(1, 0)
     far(0, 2)
-    near(0, 3)
+    far(0, 3)
     own(1, 1)
-    far(0, 3)
-    relay(1, 0)
     settle(0)
-
-    events = {
-        1: [(near, 0), (own, 2)],
-        3: [(far, 0), (relay, 1)],
-        5: [(near, 1), (own, 3)],
-        7: [(far, 1), (relay, 2)],
-    }
+    own(1, 2)
+    table_loads[2].wait()
     for pair in range(depth // 2):
         lines(0, 2 * pair)
-        for event, j in events.get(pair, []):
-            event(1, j)
+    own(1, 3)
     for s in range(slabs):
         cross_load(s).wait()
 
-    gather(0, slab_a)
+    events = (
+        ((far, 0), (relay, 1), (near, 1)),
+        ((relay, 2), (near, 2), (far, 1), (relay, 3), (near, 3)),
+        ((far, 2), (far, 3)),
+    )
 
     def steps(r, i):
         gather(2 * i + 1, slab_b)
@@ -490,26 +526,27 @@
 
     def early(i, carry):
         steps(0, i)
+        for at, batch in enumerate(events):
+
+            @pl.when(i == at)
+            def _():
+                for event, j in batch:
+                    event(1, j)
+
         return carry
 
     def late(i, carry):
-        steps(1, i)
+        steps(1, 2 * i)
+        steps(1, 2 * i + 1)
         return carry
 
-    lax.fori_loop(0, 1, early, 0)
-    near(1, 2)
-    relay(1, 3)
-    lax.fori_loop(1, 2, early, 0)
-    far(1, 2)
-    near(1, 3)
-    lax.fori_loop(2, 3, early, 0)
-    far(1, 3)
-    lax.fori_loop(3, slabs // 2, early, 0)
+    gather(0, slab_a)
+    lax.fori_loop(0, slabs // 2, early, 0)
     settle(1)
     for pair in range(depth // 2):
         lines(1, 2 * pair)
     gather(0, slab_a)
-    lax.fori_loop(0, slabs // 2, late, 0)
+    lax.fori_loop(0, slabs // 4, late, 0)
 
     for r in range(rounds):
         for j in range(narrow):
@@ -534,36 +571,44 @@
     slots = 4
     z_table = complex_table(*base_tables(KZ, width, G, -(KZ // 2))).reshape(2 * KZ, 2 * width)
     cosine, sine = base_tables(G, width, G, -(G // 2))
-    line_table = complex_table(cosine, sine).reshape(2 * G, 2, narrow, block_y)
-    line_table = line_table.transpose(0, 2, 1, 3).reshape(2 * G, 2 * width)
-    row_table = np.stack([cosine, sine], axis=0).astype(np.float32).reshape(2, G, wide, rounds, strip)
+    line_table = complex_table(cosine[: G // 2], sine[: G // 2]).reshape(G, 2, narrow, block_y // 2, 2)
+    line_table = line_table.transpose(4, 0, 2, 1, 3)
+    swapped = line_table[1].reshape(G, narrow // 2, 2, lanes // 2)[:, :, ::-1]
+    line_table = np.stack([line_table[0].reshape(G, width), swapped.reshape(G, width)])
+    row_table = np.stack([cosine, sine], axis=0).reshape(2, G, wide, rounds, strip)
     row_table = row_table.transpose(3, 0, 1, 2, 4).reshape(2 * rounds, G, wide * strip)
     hbm = pl.BlockSpec(memory_space=pl.ANY)
     vmem = pl.BlockSpec(memory_space=pltpu.VMEM)
-    smem = pl.BlockSpec(memory_space=pltpu.SMEM)
     dma = pltpu.SemaphoreType.DMA
     half = wide * strip
     out = pl.pallas_call(
-        functools.partial(fused_kernel, (depth, G, 512 if samples % 512 == 0 else samples)),
+        functools.partial(fused_kernel, (depth, G, TILE if samples % TILE == 0 else samples)),
         out_shape=jax.ShapeDtypeStruct((slabs, 2, samples), jnp.float32),
-        in_specs=[hbm, smem, vmem, smem, hbm, hbm, hbm, hbm, hbm],
+        in_specs=[hbm] * 8,
         out_specs=vmem,
         scratch_shapes=[
+            pltpu.SMEM(deapodization.shape, jnp.float32),
+            pltpu.VMEM(deapodization.shape, jnp.float32),
+            pltpu.SMEM(offsets.shape, jnp.int32),
             pltpu.VMEM(image.shape, jnp.bfloat16),
             pltpu.VMEM((block_y, width), jnp.float32),
+            pltpu.VMEM((width, width), jnp.bfloat16),
             pltpu.VMEM((KZ * (depth + 1), lanes), jnp.float32),
             pltpu.VMEM((rounds, narrow, depth, strip, lanes), jnp.bfloat16),
             pltpu.VMEM((rounds, narrow, wide, depth, strip, lanes), jnp.bfloat16),
             pltpu.VMEM(z_table.shape, jnp.bfloat16),
             pltpu.VMEM(line_table.shape, jnp.bfloat16),
+            pltpu.VMEM(row_table.shape, jnp.bfloat16),
             pltpu.VMEM(row_table.shape, jnp.float32),
             pltpu.VMEM((slots, samples, BX), jnp.bfloat16),
+            pltpu.VMEM((BX, 2 * width), jnp.bfloat16),
             pltpu.VMEM((BX, 2 * width), jnp.bfloat16),
             pltpu.VMEM((slabs, samples, 2 * width), jnp.bfloat16),
             pltpu.VMEM((slabs, samples, cells), jnp.bfloat16),
             pltpu.VMEM((2, G * (depth + 1), half), jnp.float32),
             pltpu.VMEM((cells, 2 * half), jnp.bfloat16),
             pltpu.VMEM((cells, 2 * half), jnp.bfloat16),
+            dma((3,)),
             dma((rounds,)),
             dma((3,)),
             dma((slots,)),
@@ -578,10 +623,10 @@
             dma((rounds, narrow, 4)),
         ],
         compiler_params=pltpu.CompilerParams(
-            vmem_limit_bytes=67043328, collective_id=1, has_side_effects=True
+            vmem_limit_bytes=67043328 - 100 * 1024, collective_id=1, has_side_effects=True
         ),
     )(
-        image, deapodization, deapodization, offsets, jnp.asarray(z_table), jnp.asarray(line_table),
+        image, deapodization, offsets, jnp.asarray(z_table), jnp.asarray(line_table),
         jnp.asarray(row_table), x_weight[0], cross_weight[0],
     )
     return out[None]

time: 56.9 us -> 44.6 us (0.78)
  Pallas kernels: 55.2 us -> 42.9 us
    pallas_call x1, Pallas kernels: 55.2 us -> 42.9 us  [fused_device(): pl.pallas_call(functools.partial(fused_kernel, (depth, G, TILE if samples...]
where the time goes in v2:
time: 44.6 us; the launch traced here: 44.4 us
  Pallas kernels  42.9 us (96%)
  local copies, waits for them, and re-layouts  1.54 us (3%)
    pallas_call x1, Pallas kernels, fused_device(): pl.pallas_call(functools.partial(fused_kernel, (depth, G, TILE if samples...  42.9 us
    unnamed x1, local copies, waits for them, and re-layouts  1.54 us

profile of v2, /device:TPU:0, one launch (start us, length us, event | category | flops | bytes accessed | tf_op | source)
XLA Modules:
  0.0 44.4 jit_solution(8975650400864147294)
XLA Ops:
  0.0 42.9 %shard_map.82 = f32[8,2,1536]{2,1,0:T(2,128)} custom-call(bf16[2,32,64,256]{3,2,1,0:T(8,128)(2,1)} %image_hbm.1, f32[3,256]{1,0:T(4,128)} %deap_hbm.1, s32[1,8]{1,0:T(1,128)} %offsets_hbm.1, bf16[128,512]{1,0:T(8,128)(2,1)} %constant.6.clone.z_hbm, bf16[2,512,256]{2,1,0:T(8,128)(2,1)} %constant.7.clone.line_hbm, bf16[4,512,128]{2,1,0:T(8,128)(2,1)} %constant.8.clone.row_hbm, ...), custom_call_target="tpu_custom_call" | custom-call | tf_op jit(solution)/shard_map/pallas_call | solution.py:584
  42.9 1.5 %copy.10 = f32[1,8,2,1536]{3,2,1,0:T(2,128)} copy(f32[1,8,2,1536]{3,2,1,0:T(2,128)} %bitcast.5) | data formatting | bytes 196608

commit v3 on v2

--- a/solution.py
+++ b/solution.py
@@ -254,7 +254,7 @@
     corner = across + along - w
     sibling = w + 1 - 2 * core
     held = (w, first, second, corner)
-    straight = ((0, 3),)
+    straight = ((0, 3), (1, 3))
     sib_across = across + 1 - 2 * core
     sib_along = along + 1 - 2 * core
     sib_first = sib_along + core * (sib_across - sib_along)
@@ -514,8 +514,8 @@
 
     events = (
         ((far, 0), (relay, 1), (near, 1)),
-        ((relay, 2), (near, 2), (far, 1), (relay, 3), (near, 3)),
-        ((far, 2), (far, 3)),
+        ((relay, 2), (near, 2), (relay, 3), (near, 3)),
+        ((far, 1), (far, 2), (far, 3)),
     )
 
     def steps(r, i):
@@ -583,7 +583,7 @@
     half = wide * strip
     out = pl.pallas_call(
         functools.partial(fused_kernel, (depth, G, TILE if samples % TILE == 0 else samples)),
-        out_shape=jax.ShapeDtypeStruct((slabs, 2, samples), jnp.float32),
+        out_shape=pltpu.VMEM((slabs, 2, samples), jnp.float32),
         in_specs=[hbm] * 8,
         out_specs=vmem,
         scratch_shapes=[
@@ -623,7 +623,7 @@
             dma((rounds, narrow, 4)),
         ],
         compiler_params=pltpu.CompilerParams(
-            vmem_limit_bytes=67043328 - 100 * 1024, collective_id=1, has_side_effects=True
+            vmem_limit_bytes=67043328 - 300 * 1024, collective_id=1, has_side_effects=True
         ),
     )(
         image, deapodization, offsets, jnp.asarray(z_table), jnp.asarray(line_table),

time: 44.6 us -> 42.2 us (0.946)
  Pallas kernels: 42.9 us -> 41.4 us
  local copies, waits for them, and re-layouts: 1.54 us -> 0.64 us
    pallas_call x1, Pallas kernels: 42.9 us -> 41.4 us  [fused_device(): pl.pallas_call(functools.partial(fused_kernel, (depth, G, TILE if samples...]
    unnamed x1, local copies, waits for them, and re-layouts: 1.54 us -> 0.64 us
where the time goes in v3:
time: 42.2 us; the launch traced here: 42.1 us
  Pallas kernels  41.4 us (98%)
  local copies, waits for them, and re-layouts  0.64 us (2%)
    pallas_call x1, Pallas kernels, fused_device(): pl.pallas_call(functools.partial(fused_kernel, (depth, G, TILE if samples...  41.4 us

profile of v3, /device:TPU:0, one launch (start us, length us, event | category | flops | bytes accessed | tf_op | source)
XLA Modules:
  0.0 42.1 jit_solution(6682275657059384914)
XLA Ops:
  0.0 41.4 %shard_map.82 = f32[8,2,1536]{2,1,0:T(2,128)S(1)} custom-call(bf16[2,32,64,256]{3,2,1,0:T(8,128)(2,1)} %image_hbm.1, f32[3,256]{1,0:T(4,128)} %deap_hbm.1, s32[1,8]{1,0:T(1,128)} %offsets_hbm.1, bf16[128,512]{1,0:T(8,128)(2,1)} %constant.6.clone.z_hbm, bf16[2,512,256]{2,1,0:T(8,128)(2,1)} %constant.7.clone.line_hbm, ...), custom_call_target="tpu_custom_call" | custom-call | tf_op jit(solution)/shard_map/pallas_call | solution.py:584
  41.4 0.6 %copy.10 = f32[1,8,2,1536]{3,2,1,0:T(2,128)} copy(f32[1,8,2,1536]{3,2,1,0:T(2,128)S(1)} %bitcast.3) | data formatting | bytes 196608

commit v4 on v3

--- a/solution.py
+++ b/solution.py
@@ -229,7 +229,7 @@
 
 def fused_kernel(
     sizes, image_hbm, deap_hbm, offsets_hbm, z_hbm, line_hbm, row_hbm, x_hbm, cross_hbm, out_ref,
-    deap_smem, deap_ref, offsets_ref, image_ref, scale_ref, perm_ref, spread_ref, send_ref, grid_ref, z_ref, line_ref, packed_ref, row_ref, x_ref, window_a, window_b, gain_ref,
+    deap_smem, deap_ref, offsets_ref, image_ref, perm_ref, spread_ref, send_ref, grid_ref, z_ref, line_ref, packed_ref, row_ref, x_ref, window_a, window_b, gain_ref,
     cross_ref, wide_ref, slab_a, slab_b,
     small_sem, image_sem, table_sem, x_sem, cross_sem,
     swap_send, swap_recv, own_send, near_recv, relay_send, relay_recv, pass_send, pass_recv,
@@ -240,7 +240,7 @@
     rounds, narrow, wide, _, strip, lanes = grid_ref.shape
     windows = (window_a, window_b)
     slots = x_ref.shape[0]
-    block_y, width = scale_ref.shape
+    block_y, width = lanes // 2, perm_ref.shape[0]
     slabs, samples, cells = cross_ref.shape
     pitch = depth + 1
     half = wide * strip
@@ -309,8 +309,9 @@
     for copy in small_loads:
         copy.wait()
     last = deap_ref[2:3, :]
-    for y in range(block_y):
-        scale_ref[y : y + 1, :] = last * deap_smem[1, n * block_y + y]
+    lane = lax.broadcasted_iota(jnp.int32, (8, lanes), 1)
+    middle = pltpu.roll(jnp.broadcast_to(deap_ref[1:2, :], (8, width)), width - n * block_y, 1)[:, :lanes]
+    middle = jnp.where(lane < block_y, middle, pltpu.roll(middle, block_y, 1))
 
     def band(r):
         quarter = block_y // 2
@@ -321,12 +322,16 @@
         for c in range(2):
             pieces = []
             for x in range(strip):
-                gain = scale_ref[...] * deap_smem[0, w * rounds * strip + r * strip + x]
-                pieces.append((image_ref[c, r * strip + x].astype(jnp.float32) * gain).astype(jnp.bfloat16))
+                pieces.append((image_ref[c, r * strip + x].astype(jnp.float32) * last).astype(jnp.bfloat16))
             halves.append(jnp.concatenate(pieces, axis=0))
         both = jnp.concatenate(halves, axis=1)
         value = lax.dot_general(z_ref[...], both, (((1,), (1,)), ((), ())), preferred_element_type=jnp.float32)
-        value = value.astype(jnp.bfloat16)
+        start = (w * rounds + r) * strip
+        scales = [
+            middle * jnp.where(lane < block_y, deap_smem[0, start + x], deap_smem[0, start + x + 1])
+            for x in range(0, strip, 2)
+        ]
+        value = (value * jnp.concatenate(scales, axis=1)[:1]).astype(jnp.bfloat16)
         value = jnp.concatenate([value[:, at : at + width] for at in range(0, strip * block_y, width)], axis=0)
         value = jnp.dot(value, perm_ref[...], preferred_element_type=jnp.float32)
         for at in range(0, strip, group):
@@ -480,19 +485,19 @@
     table_loads[1].wait()
     row_ref[...] = packed_ref[...].astype(jnp.float32)
     gains(0, 1)
+    gains(2, 3)
     relay(0, 0)
     own(0, 1)
-    gains(2, 3)
     near(0, 0)
+    gains(4, 5)
     own(0, 2)
-    gains(4, 5)
+    gains(6, 7)
     own(0, 3)
     for j in range(1, narrow):
         swap(1, j).start()
     relay(0, 1)
+    far(0, 0)
     near(0, 1)
-    far(0, 0)
-    gains(6, 7)
     relay(0, 2)
     near(0, 2)
     relay(0, 3)
@@ -513,8 +518,7 @@
         cross_load(s).wait()
 
     events = (
-        ((far, 0), (relay, 1), (near, 1)),
-        ((relay, 2), (near, 2), (relay, 3), (near, 3)),
+        ((far, 0), (relay, 1), (near, 1), (relay, 2), (near, 2), (relay, 3), (near, 3)),
         ((far, 1), (far, 2), (far, 3)),
     )
 
@@ -525,7 +529,8 @@
         contract(r, 2 * i + 1, slab_b)
 
     def early(i, carry):
-        steps(0, i)
+        steps(0, 2 * i)
+        steps(0, 2 * i + 1)
         for at, batch in enumerate(events):
 
             @pl.when(i == at)
@@ -541,7 +546,7 @@
         return carry
 
     gather(0, slab_a)
-    lax.fori_loop(0, slabs // 2, early, 0)
+    lax.fori_loop(0, slabs // 4, early, 0)
     settle(1)
     for pair in range(depth // 2):
         lines(1, 2 * pair)
@@ -568,7 +573,7 @@
     rounds = 2
     strip = block_x // rounds
     lanes = 2 * block_y
-    slots = 4
+    slots = slabs
     z_table = complex_table(*base_tables(KZ, width, G, -(KZ // 2))).reshape(2 * KZ, 2 * width)
     cosine, sine = base_tables(G, width, G, -(G // 2))
     line_table = complex_table(cosine[: G // 2], sine[: G // 2]).reshape(G, 2, narrow, block_y // 2, 2)
@@ -591,7 +596,6 @@
             pltpu.VMEM(deapodization.shape, jnp.float32),
             pltpu.SMEM(offsets.shape, jnp.int32),
             pltpu.VMEM(image.shape, jnp.bfloat16),
-            pltpu.VMEM((block_y, width), jnp.float32),
             pltpu.VMEM((width, width), jnp.bfloat16),
             pltpu.VMEM((KZ * (depth + 1), lanes), jnp.float32),
             pltpu.VMEM((rounds, narrow, depth, strip, lanes), jnp.bfloat16),

time: 42.2 us -> 42.1 us (level)
  no operation moved by 1% of the time
where the time goes in v4:
time: 42.1 us; the launch traced here: 41.9 us
  Pallas kernels  41.3 us (98%)
  local copies, waits for them, and re-layouts  0.64 us (2%)
    pallas_call x1, Pallas kernels, fused_device(): pl.pallas_call(functools.partial(fused_kernel, (depth, G, TILE if samples...  41.3 us

profile of v4, /device:TPU:0, one launch (start us, length us, event | category | flops | bytes accessed | tf_op | source)
XLA Modules:
  0.0 41.9 jit_solution(15556637074582135482)
XLA Ops:
  0.0 41.3 %shard_map.82 = f32[8,2,1536]{2,1,0:T(2,128)S(1)} custom-call(bf16[2,32,64,256]{3,2,1,0:T(8,128)(2,1)} %image_hbm.1, f32[3,256]{1,0:T(4,128)} %deap_hbm.1, s32[1,8]{1,0:T(1,128)} %offsets_hbm.1, bf16[128,512]{1,0:T(8,128)(2,1)} %constant.6.clone.z_hbm, bf16[2,512,256]{2,1,0:T(8,128)(2,1)} %constant.7.clone.line_hbm, ...), custom_call_target="tpu_custom_call" | custom-call | tf_op jit(solution)/shard_map/pallas_call | solution.py:589
  41.3 0.6 %copy.10 = f32[1,8,2,1536]{3,2,1,0:T(2,128)} copy(f32[1,8,2,1536]{3,2,1,0:T(2,128)S(1)} %bitcast.3) | data formatting | bytes 196608
